TPU v7x, 32 devices: a whole 2x2x4 slice. The times are simulated.
32 devices in a mesh: dp: 8 (over y, x, core), mp: 4 (over z).
Axes of the slice: x: 2, y: 2, z: 4, core: 2. Of those that a mesh axis runs over, the one named last changes fastest.
Arguments:
- slab_values: bfloat16 [32, 32, 2048], P(('dp', 'mp')), may hold values from -6 to 6
- row_ids: int32 [32, 32, 32], P(('dp', 'mp')), may hold values from 0 to 4095, as said below
- peer_counts: int32 [32, 32], P(('dp', 'mp')), may hold values from 1 to 32, as said below
- lookup_slots: int32 [8192, 16], P(('dp', 'mp')), may hold values from 0 to 1023, as said below
- labels: int32 [8192], P('dp'), may hold values 0 or 1
- sample_weight: float32 [8192], P('dp'), may hold values from 0.3 to 9
- weight_in: bfloat16 [1024, 8192], P(None, 'mp'), may hold values from -0.1875 to 0.1875
- bias_in: float32 [8192], P('mp'), may hold values from -3 to 3
- weight_out: bfloat16 [8192], P('mp'), may hold values from -0.0625 to 0.0625
- dense_accum: float32 [1024, 8192], P('dp', 'mp'), may hold values from 1e-08 to 1e-06
- table_rows: float32 [131072, 64], P(('dp', 'mp')), may hold values from -0.12 to 0.12
- table_accum: float32 [131072], P(('dp', 'mp')), may hold values from 1e-12 to 1e-05
Outputs:
- weight_new: bfloat16 [1024, 8192], P(None, 'mp')
- accum_new: float32 [1024, 8192], P('dp', 'mp')
- table_new: float32 [131072, 64], P(('dp', 'mp'))
- table_accum_new: float32 [131072], P(('dp', 'mp'))
Inputs may be any that keep to these rules, and one draw needn't show every extreme that they name: `row_ids`: the first peer_counts entries of each device's list for an owner are distinct rows of that owner's shard. `peer_counts`: some owner has 32 touched rows on every device, and some device has 32 touched rows of every owner. `lookup_slots`: below the sum of that device's peer_counts; every device has a lookup of its last touched row.
All inputs are finite; a program needn't handle non-finite values. No bound on the sum of `labels` on one device may be relied on, other than what follows from the above.
Results may differ from a plain program's by a relative error of at most 0.0034.
Values may be sent and summed in bfloat16 or wider, within the bound.
A program may use at most 128 MiB of HBM per device.

v0:
```python
import jax
import jax.numpy as jnp
from jax import lax
from jax.sharding import PartitionSpec as P

clip_norm = 1.0
dense_rate = 0.02
table_rate = 0.5
adagrad_eps = 1e-10


def slot_index(compact, counts, capacity):
    slot_ends = jnp.cumsum(counts)
    owner_index = jnp.sum((compact[..., None] >= slot_ends).astype(jnp.int32), axis=-1)
    slot_starts = slot_ends - counts
    owner_match = owner_index[..., None] == jnp.arange(counts.shape[0], dtype=jnp.int32)
    owner_begin = jnp.sum(jnp.where(owner_match, slot_starts, 0), axis=-1)
    return owner_index * capacity + compact - owner_begin


def body(
    slab_values,
    row_ids,
    peer_counts,
    lookup_slots,
    labels,
    sample_weight,
    weight_in,
    bias_in,
    weight_out,
    dense_accum,
    table_rows,
    table_accum,
):
    peers = peer_counts.shape[1]
    capacity = row_ids.shape[2]
    emb_width = slab_values.shape[2] // capacity
    batch = lookup_slots.shape[0]
    features = lookup_slots.shape[1]
    index = slot_index(lookup_slots, peer_counts[0], capacity)
    slab_view = slab_values[0].reshape(peers * capacity, emb_width)
    pooled = slab_view[index].reshape(batch, features * emb_width)
    group = lax.all_gather(pooled, "mp", axis=0, tiled=True)
    act = jnp.dot(group, weight_in, preferred_element_type=jnp.float32) + bias_in
    hidden = jax.nn.silu(act).astype(jnp.bfloat16)
    logit = lax.psum(jnp.dot(hidden, weight_out, preferred_element_type=jnp.float32), "mp")
    dlogit = sample_weight * (jax.nn.sigmoid(logit) - labels.astype(jnp.float32))
    sigma = jax.nn.sigmoid(act)
    dact = (
        dlogit[:, None]
        * weight_out.astype(jnp.float32)[None, :]
        * sigma
        * (1.0 + act * (1.0 - sigma))
    ).astype(jnp.bfloat16)
    dpooled = lax.psum_scatter(
        lax.dot_general(
            dact, weight_in, (((1,), (1,)), ((), ())), preferred_element_type=jnp.float32
        ),
        "mp",
        scatter_dimension=0,
        tiled=True,
    )
    slot_grad = jax.ops.segment_sum(
        dpooled.reshape(batch * features, emb_width),
        index.reshape(-1),
        num_segments=peers * capacity,
    )
    grad_in = lax.dot_general(
        group, dact, (((0,), (0,)), ((), ())), preferred_element_type=jnp.float32
    )
    grad_bias = jnp.sum(dact.astype(jnp.float32), axis=0)
    grad_out = jnp.dot(dlogit, hidden.astype(jnp.float32), precision=lax.Precision.HIGHEST)
    first_group = (lax.axis_index("dp") == 0).astype(jnp.float32)
    own_rows = dense_accum.shape[0]
    row_start = lax.axis_index("dp") * own_rows
    grad_rows = lax.psum_scatter(grad_in, "dp", scatter_dimension=0, tiled=True)
    grad_bias, grad_out = lax.psum((grad_bias, grad_out), "dp")
    dense_square = jnp.sum(grad_rows * grad_rows)
    dense_square = dense_square + first_group * (
        jnp.sum(grad_bias * grad_bias) + jnp.sum(grad_out * grad_out)
    )
    total = lax.psum(dense_square + jnp.sum(slot_grad * slot_grad), ("dp", "mp"))
    scale = clip_norm / jnp.maximum(jnp.sqrt(total), clip_norm)
    clipped = scale * grad_rows
    accum_new = dense_accum + clipped * clipped
    weight_part = lax.dynamic_slice_in_dim(weight_in, row_start, own_rows, 0).astype(jnp.float32)
    updated = (weight_part - dense_rate * clipped / (jnp.sqrt(accum_new) + adagrad_eps)).astype(
        jnp.bfloat16
    )
    weight_new = lax.all_gather(updated, "dp", axis=0, tiled=True)
    row_values = row_ids[0].astype(jnp.float32)
    outgoing = (scale * slot_grad).reshape(peers, capacity * emb_width)
    arrived, arrived_rows = (
        lax.all_to_all(outgoing, ("dp", "mp"), split_axis=0, concat_axis=0, tiled=True),
        lax.all_to_all(row_values, ("dp", "mp"), split_axis=0, concat_axis=0, tiled=True),
    )
    received = jax.ops.segment_sum(
        arrived.reshape(-1, emb_width),
        arrived_rows.reshape(-1).astype(jnp.int32),
        num_segments=table_rows.shape[0],
    )
    table_accum_new = table_accum + jnp.mean(received * received, axis=1)
    table_new = table_rows - table_rate * received / (
        jnp.sqrt(table_accum_new)[:, None] + adagrad_eps
    )
    return (weight_new, accum_new, table_new, table_accum_new)


def solution(mesh):
    placed = (
        P(("dp", "mp"), None, None),
        P(("dp", "mp"), None, None),
        P(("dp", "mp"), None),
        P(("dp", "mp"), None),
        P("dp"),
        P("dp"),
        P(None, "mp"),
        P("mp"),
        P("mp"),
        P("dp", "mp"),
        P(("dp", "mp"), None),
        P(("dp", "mp")),
    )
    return jax.shard_map(
        body,
        mesh=mesh,
        in_specs=placed,
        out_specs=(P(None, "mp"), P("dp", "mp"), P(("dp", "mp"), None), P(("dp", "mp"))),
        check_vma=False,
    )
```

profile of v0, /device:TPU:0, one launch (start us, length us, event | category | flops | bytes accessed | tf_op | source)
XLA Modules:
  0.0 362.3 jit_solution(8915836303579359678)
XLA Ops:
  10.8 1.2 reshape_squeeze.3
  12.0 12.1 %gather_fusion = bf16[4096,64]{1,0:T(8,128)(2,1)S(1)} fusion(bf16[1024,64]{1,0:T(8,128)(2,1)S(1)} %reshape_squeeze.3, s32[4096]{0:T(1024)S(1)} %broadcast_clamp_fusion), kind=kCustom, calls=%fused_computation | custom fusion | bytes 1064960 | tf_op jit(solution)/shard_map/gather | solution.py:42
  24.1 1.5 reshape.81
  25.7 48.4 %all-gather.3.cloned.1.call-done = bf16[1024,1024]{1,0:T(8,128)(2,1)} async-done(((bf16[256,1024]{1,0:T(8,128)(2,1)}), bf16[1024,1024]{1,0:T(8,128)(2,1)}) %all-gather.3.cloned.1.call-update) | async-done | bytes 2097168 | tf_op jit(solution)/shard_map/all_gather | solution.py:43
  74.2 11.2 %multiply_convert_fusion.1 = (bf16[1024,2048]{1,0:T(8,128)(2,1)S(1)}, f32[1024,2048]{1,0:T(8,128)}) fusion(f32[2048]{0:T(1024)S(1)} %copy-done.7, bf16[1024,1024]{1,0:T(8,128)(2,1)} %all-gather.3.cloned.1.call-done, bf16[1024,2048]{1,0:T(8,128)(2,1)} %param.18), kind=kOutput, calls=%fused_computation.5 | convolution fusion | flops 4307550208 | bytes 18882560 | tf_op jit(solution)/shard_map/dot_general | solution.py:44
  85.3 2.0 copy-done
  87.3 1.2 fusion.4
  88.5 9.7 %psum.28 = f32[1024]{0:T(1024)S(1)} all-reduce(f32[1024]{0:T(1024)S(1)} %bitcast.19), channel_id=1, replica_groups=mesh['dp'=8,'mp'=4] {'mp'}, use_global_device_ids=true, to_apply=%region_3.4 | all-reduce | flops 1024 | bytes 8192 | tf_op jit(solution)/shard_map/psum | solution.py:46
  98.3 6.1 %convert_reduce_fusion = (f32[2048]{0:T(1024)S(1)}, bf16[1024,2048]{1,0:T(8,128)(2,1)S(1)}) fusion(f32[1024,2048]{1,0:T(8,128)} %get-tuple-element.27, f32[2048]{0:T(1024)S(1)} %copy-done.7, f32[2048]{0:T(1024)S(1)} %convert_element_type.56, f32[1024]{0:T(1024)S(1)} %subtract_multiply_fusion), kind=kLoop, calls=%fused_computation.3 | loop fusion | flops 27260928 | bytes 12611584 | tf_op jit(solution)/shard_map/reduce_sum | solution.py:71
  104.4 2.0 copy-done.1
  106.4 6.1 %fusion.7 = f32[1024,1024]{1,0:T(8,128)} fusion(bf16[1024,2048]{1,0:T(8,128)(2,1)S(1)} %get-tuple-element.23, bf16[1024,2048]{1,0:T(8,128)(2,1)S(1)} %copy-done.3), kind=kOutput, calls=%fused_computation.34 | convolution fusion | flops 4294967296 | bytes 12582912 | tf_op jit(solution)/shard_map/dot_general | solution.py:56
  112.7 1.3 copy-done.10
  114.1 9.0 %fusion.5 = f32[1024,2048]{1,0:T(8,128)} fusion(bf16[1024,1024]{1,0:T(8,128)(2,1)S(1)} %copy-done.10, bf16[1024,2048]{1,0:T(8,128)(2,1)} %copy-done.1), kind=kOutput, calls=%fused_computation.32 | convolution fusion | flops 4294967296 | bytes 14680064 | tf_op jit(solution)/shard_map/dot_general | solution.py:68
  123.3 3.9 %fusion.6 = f32[1,2048]{1,0:T(1,128)S(1)} fusion(f32[1024,1]{0,1:T(1,128)S(1)} %bitcast.17, bf16[1024,2048]{1,0:T(8,128)(2,1)} %copy-done), kind=kOutput, calls=%fused_computation.33 | convolution fusion | flops 25165824 | bytes 4206592 | tf_op jit(solution)/shard_map/dot_general | solution.py:72
  127.2 22.7 %all-reduce = (f32[2048]{0:T(1024)S(1)}, f32[2048]{0:T(1024)S(1)}) all-reduce(f32[2048]{0:T(1024)S(1)} %get-tuple-element.22, f32[2048]{0:T(1024)S(1)} %bitcast.18), channel_id=1, replica_groups=mesh['dp'=8,'mp'=4] {'dp'}, use_global_device_ids=true, to_apply=%region_7.8 | all-reduce | flops 4096 | bytes 32768 | tf_op jit(solution)/shard_map/psum | solution.py:77
  151.9 35.8 %reduce-scatter.5.cloned.1.call-done = f32[256,1024]{1,0:T(8,128)} async-done(((f32[1024,1024]{1,0:T(8,128)}), f32[256,1024]{1,0:T(8,128)}) %reduce-scatter.5.cloned.1.call-update) | async-done | bytes 1048592 | tf_op jit(solution)/shard_map/reduce_scatter | solution.py:55
  187.7 1.7 reshape.96
  189.4 22.5 %scatter_custom_fusion = f32[1024,64]{1,0:T(8,128)S(1)} fusion(s32[4096]{0:T(1024)S(1)} %reshape.94, f32[4096,64]{1,0:T(8,128)S(1)} %reshape.96, f32[]{:T(128)} %constant.19.clone.1), kind=kCustom, calls=%fused_computation.19 | custom fusion | flops 262144 | bytes 262148 | tf_op jit(solution)/shard_map/scatter-add | solution.py:63
  212.6 50.6 %reduce-scatter.3.cloned.1.call-done = f32[128,2048]{1,0:T(8,128)} async-done(((f32[1024,2048]{1,0:T(8,128)}), f32[128,2048]{1,0:T(8,128)}) %reduce-scatter.3.cloned.1.call-update) | async-done | bytes 1048592 | tf_op jit(solution)/shard_map/reduce_scatter | solution.py:76
  263.2 2.1 multiply_reduce_fusion.1
  266.6 39.3 %psum.31 = f32[]{:T(128)} all-reduce(f32[]{:T(128)S(6)} %add.86), channel_id=1, replica_groups=mesh['dp'=8,'mp'=4] {'dp','mp'}, use_global_device_ids=true, to_apply=%region_14.15 | all-reduce | flops 1 | bytes 8 | tf_op jit(solution)/shard_map/psum | solution.py:82
  306.6 3.4 subtract_convert_fusion
  310.7 5.6 %all-to-all-start = ((f32[32,1,32]{2,1,0:T(1,128)}), f32[32,1,32]{2,1,0:T(1,128)S(1)}, u32[]{:S(2)}, u32[]{:S(2)}) async-start(f32[32,1,32]{2,1,0:T(1,128)} %bitcast.5), calls=%async_computation.2 | async-start | bytes 32768 | tf_op jit(solution)/shard_map/all_to_all | solution.py:95
  316.3 1.0 all_to_all.13
  317.3 6.1 %all-to-all-done = f32[32,1,32]{2,1,0:T(1,128)S(1)} async-done(((f32[32,1,32]{2,1,0:T(1,128)}), f32[32,1,32]{2,1,0:T(1,128)S(1)}, u32[]{:S(2)}, u32[]{:S(2)}) %all-to-all-start) | async-done | bytes 4128 | tf_op jit(solution)/shard_map/all_to_all | solution.py:95
  323.4 2.8 all-to-all-start.1
  326.2 1.9 copy.38
  328.3 8.0 %all-to-all-done.1 = f32[32,1,2048]{2,1,0:T(1,128)S(1)} async-done(((f32[32,1,2048]{2,1,0:T(1,128)}), f32[32,1,2048]{2,1,0:T(1,128)S(1)}, u32[]{:S(2)}, u32[]{:S(2)}) %all-to-all-start.1) | async-done | bytes 262176 | tf_op jit(solution)/shard_map/all_to_all | solution.py:94
  337.1 6.5 %scatter_custom_fusion.1 = f32[4096,64]{1,0:T(8,128)S(1)} fusion(s32[1024]{0:T(1024)S(1)} %reshape.102, f32[1024,64]{1,0:T(8,128)S(1)} %reshape.104, f32[]{:T(128)} %constant.19.clone.1), kind=kCustom, calls=%fused_computation.9 | custom fusion | flops 65536 | bytes 1048580 | tf_op jit(solution)/shard_map/scatter-add | solution.py:97
  344.9 2.9 divide_subtract_fusion
  347.8 3.1 copy.39
  351.0 4.8 %copy.41 = bf16[1024,2048]{1,0:T(8,128)(2,1)} copy(bf16[1024,2048]{1,0:T(8,128)(2,1)} %all-gather.5.cloned.1.call-done) | data formatting | bytes 8388608
  (53 shorter events, 8.4 us)
Async XLA Ops:
  7.2 67.0 %all-gather.3.cloned.1.call-start = ((), (), s32[]{:S(2)}) async-start(), calls=%async_computation.4 | async-start | bytes 2621440 | tf_op jit(solution)/shard_map/all_gather | solution.py:43
  11.9 13.8 %copy-start.4 = (bf16[2048]{0:T(1024)(128)(2,1)S(1)}, bf16[2048]{0:T(1024)(128)(2,1)}, u32[]{:S(2)}) copy-start(bf16[2048]{0:T(1024)(128)(2,1)} %param.20) | copy-start | bytes 12292
  12.0 62.2 %copy-start.7 = (f32[2048]{0:T(1024)S(1)}, f32[2048]{0:T(1024)}, u32[]{:S(2)}) copy-start(f32[2048]{0:T(1024)} %param.19) | copy-start | bytes 24580
  25.7 162.0 %reduce-scatter.5.cloned.1.call-start = ((), (), s32[]{:S(2)}) async-start(), calls=%async_computation.6 | async-start | bytes 5242880 | tf_op jit(solution)/shard_map/reduce_scatter | solution.py:55
  85.3 2.0 copy-start
  85.3 12.9 %copy-start.8 = (f32[1024]{0:T(1024)S(1)}, f32[1024]{0:T(1024)}, u32[]{:S(2)}) copy-start(f32[1024]{0:T(1024)} %param.17) | copy-start | bytes 12292
  85.3 12.9 %copy-start.9 = (s32[1024]{0:T(1024)S(1)}, s32[1024]{0:T(1024)}, u32[]{:S(2)}) copy-start(s32[1024]{0:T(1024)} %param.16) | copy-start | bytes 12292
  98.2 8.1 %copy-start.3 = (bf16[1024,2048]{1,0:T(8,128)(2,1)S(1)}, bf16[1024,2048]{1,0:T(8,128)(2,1)}, u32[]{:S(2)}) copy-start(bf16[1024,2048]{1,0:T(8,128)(2,1)} %param.18) | copy-start | bytes 12582916
  104.4 2.0 copy-start.1
  112.5 1.6 copy-start.10
  112.5 150.7 %reduce-scatter.3.cloned.1.call-start = ((), (), s32[]{:S(2)}) async-start(), calls=%async_computation.5 | async-start | bytes 9437184 | tf_op jit(solution)/shard_map/reduce_scatter | solution.py:76
  123.1 227.9 %all-gather.5.cloned.1.call-start = ((), (), s32[]{:S(2)}) async-start(), calls=%async_computation.7 | async-start | bytes 4718592 | tf_op jit(solution)/shard_map/all_gather | solution.py:90
  189.4 120.7 %copy-start.5 = (s32[1,32,32]{2,1,0:T(8,128)S(1)}, s32[1,32,32]{2,1,0:T(8,128)}, u32[]{:S(2)}) copy-start(s32[1,32,32]{2,1,0:T(8,128)} %param.13) | copy-start | bytes 12292
  212.6 113.6 %copy-start.2 = (f32[4096,64]{0,1:T(8,128)S(1)}, f32[4096,64]{0,1:T(8,128)}, u32[]{:S(2)}) copy-start(f32[4096,64]{0,1:T(8,128)} %param.22) | copy-start | bytes 3145732
  310.7 12.7 %all-to-all-start = ((f32[32,1,32]{2,1,0:T(1,128)}), f32[32,1,32]{2,1,0:T(1,128)S(1)}, u32[]{:S(2)}, u32[]{:S(2)}) async-start(f32[32,1,32]{2,1,0:T(1,128)} %bitcast.5), calls=%async_computation.2 | async-start | bytes 32768 | tf_op jit(solution)/shard_map/all_to_all | solution.py:95
  323.4 12.9 %all-to-all-start.1 = ((f32[32,1,2048]{2,1,0:T(1,128)}), f32[32,1,2048]{2,1,0:T(1,128)S(1)}, u32[]{:S(2)}, u32[]{:S(2)}) async-start(f32[32,1,2048]{2,1,0:T(1,128)} %all_to_all.13), calls=%async_computation.3 | async-start | bytes 524288 | tf_op jit(solution)/shard_map/all_to_all | solution.py:94
  326.2 18.1 %copy-start.6 = (f32[4096]{0:T(1024)S(1)}, f32[4096]{0:T(1024)}, u32[]{:S(2)}) copy-start(f32[4096]{0:T(1024)} %param.23) | copy-start | bytes 49156
Sparse Core Ops, SparseCore 0:
  25.8 48.3 all-gather.2
  112.6 74.9 reduce-scatter.4
  191.1 72.0 reduce-scatter.2
  310.2 37.9 all-gather.4
where the time goes:
time: 363 us; the launch traced here: 362 us
  waiting for transfers between devices  149 us (41%)
  blocking collectives  71.8 us (20%)
  other arithmetic  50 us (14%)
  local copies, waits for them, and re-layouts  34.2 us (9%)
  matrix products  31.3 us (9%)
  between operations  17.4 us (5%)
  starting transfers between devices  8.71 us (2%)
    reduce_scatter x1, waiting for transfers between devices, body(): grad_rows = lax.psum_scatter(grad_in, 'dp', scatter_dimension=0, tiled=True)  50.6 us
    all_gather x1, waiting for transfers between devices, body(): group = lax.all_gather(pooled, 'mp', axis=0, tiled=True)  48.4 us
    psum x1, blocking collectives, body(): lax.psum(dense_square + jnp.sum(slot_grad * slot_grad), ('dp', 'mp'))  39.3 us
    reduce_scatter x1, waiting for transfers between devices, body(): lax.psum_scatter(lax.dot_general(dact, weight_in, (((1,), (1,)), ((), ())...  35.8 us
    psum x1, blocking collectives, body(): grad_bias, grad_out = lax.psum((grad_bias, grad_out), 'dp')  22.7 us
    scatter-add x1, other arithmetic, body(): jax.ops.segment_sum(dpooled.reshape(batch * features, emb_width), index.r...  22.5 us
    unnamed x26, local copies, waits for them, and re-layouts  15.2 us
    gather x1, local copies, waits for them, and re-layouts, body(): pooled = slab_view[index].reshape(batch, features * emb_width)  12.1 us
  transfers between devices with their start and end apart: 6, of which 5 were waited for; matrix products, arithmetic and copies ran while one was open for 15% of the time, Pallas kernels for 0%

commit v1 on v0

v1 whole, which is shorter than its diff:
```python
import functools

import jax
import jax.numpy as jnp
from jax import lax
from jax.experimental import pallas as pl
from jax.experimental.pallas import tpu as pltpu
from jax.sharding import PartitionSpec as P

clip_norm = 1.0
dense_rate = 0.02
table_rate = 0.5
adagrad_eps = 1e-10
MESH = pl.DeviceIdType.MESH
VMEM_BYTES = 60 * 1024 * 1024


def slot_index(compact, counts, capacity):
    slot_ends = jnp.cumsum(counts)
    owner_index = jnp.sum((compact[..., None] >= slot_ends).astype(jnp.int32), axis=-1)
    slot_starts = slot_ends - counts
    owner_match = owner_index[..., None] == jnp.arange(counts.shape[0], dtype=jnp.int32)
    owner_begin = jnp.sum(jnp.where(owner_match, slot_starts, 0), axis=-1)
    return owner_index * capacity + compact - owner_begin


def flat_place(axes, sizes):
    place = jnp.int32(0)
    for axis, size in zip(axes, sizes):
        place = place * size + lax.axis_index(axis)
    return place


def device_of(axes, sizes, place):
    where = {}
    for axis, size in reversed(list(zip(axes, sizes))):
        where[axis] = lax.rem(place, size)
        place = lax.div(place, size)
    return where


def greet(axes, sizes, me, number):
    barrier = pltpu.get_barrier_semaphore()
    for step in range(1, number):
        peer = lax.rem(me + step, number)
        pl.semaphore_signal(
            barrier, inc=1, device_id=device_of(axes, sizes, peer), device_id_type=MESH
        )
    pl.semaphore_wait(barrier, number - 1)


def exchange_kernel(axes, sizes, splits, *refs):
    count = len(splits)
    ins, outs = refs[:count], refs[count : 2 * count]
    send_sem, recv_sem = refs[2 * count :]
    number = 1
    for size in sizes:
        number *= size
    me = flat_place(axes, sizes)
    greet(axes, sizes, me, number)
    copies = []
    for step in range(1, number):
        peer = lax.rem(me + step, number)
        for i, split in enumerate(splits):
            copy = pltpu.make_async_remote_copy(
                src_ref=ins[i].at[peer] if split else ins[i],
                dst_ref=outs[i].at[me],
                send_sem=send_sem.at[i, step],
                recv_sem=recv_sem.at[i, step],
                device_id=device_of(axes, sizes, peer),
                device_id_type=MESH,
            )
            copy.start()
            copies.append(copy)
    for i, split in enumerate(splits):
        outs[i][me] = ins[i][me] if split else ins[i][...]
    for copy in copies:
        copy.wait()


def exchange(mesh, axes, arrays, splits, collective_id):
    sizes = tuple(mesh.shape[axis] for axis in axes)
    number = 1
    for size in sizes:
        number *= size
    shapes = [
        jax.ShapeDtypeStruct(a.shape if s else (number,) + a.shape, a.dtype)
        for a, s in zip(arrays, splits)
    ]
    return pl.pallas_call(
        functools.partial(exchange_kernel, axes, sizes, splits),
        out_shape=shapes,
        in_specs=[pl.BlockSpec(memory_space=pltpu.VMEM)] * len(arrays),
        out_specs=[pl.BlockSpec(memory_space=pltpu.VMEM)] * len(arrays),
        scratch_shapes=[
            pltpu.SemaphoreType.DMA((len(arrays), number)),
            pltpu.SemaphoreType.DMA((len(arrays), number)),
        ],
        compiler_params=pltpu.CompilerParams(collective_id=collective_id, has_side_effects=True),
    )(*arrays)


def bit_orders(number):
    bits = list(range(number.bit_length() - 1))
    return (bits, bits[:1] + bits[:0:-1])


def subsets(bits):
    if not bits:
        return [[]]
    rest = subsets(bits[1:])
    return rest + [[bits[0]] + r for r in rest]


def flip(place, bit):
    step = 1 << bit
    return place + step * (1 - 2 * lax.rem(lax.div(place, step), 2))


def flip_all(place, bits):
    for bit in bits:
        place = flip(place, bit)
    return place


def scatter_kernel(number, grad_ref, small_ref, out_ref, gathered_ref, *scratch):
    orders = bit_orders(number)
    phases = len(orders[0])
    gots = (scratch[:phases], scratch[phases : 2 * phases])
    sums = (scratch[2 * phases : 3 * phases - 1], scratch[3 * phases - 1 : 4 * phases - 2])
    send_sem, recv_sem, small_send, small_recv = scratch[4 * phases - 2 :]
    me = lax.axis_index("dp")
    half = out_ref.shape[0] // 2
    greet(("dp",), (number,), me, number)
    flying = [[], []]
    everything = []

    def start(phase, stream):
        order = orders[stream]
        bit, left = order[phase], order[phase + 1 :]
        kept = subsets(left)
        flying[stream] = []
        for slot, subset in enumerate(kept):
            if phase == 0:
                block = flip(flip_all(me, subset), bit)
                source = grad_ref.at[block, pl.ds(stream * half, half)]
            else:
                source = sums[stream][phase - 1].at[len(kept) + slot]
            copy = pltpu.make_async_remote_copy(
                src_ref=source,
                dst_ref=gots[stream][phase].at[slot],
                send_sem=send_sem.at[stream, phase, slot],
                recv_sem=recv_sem.at[stream, phase, slot],
                device_id={"dp": flip(me, bit)},
                device_id_type=MESH,
            )
            copy.start()
            flying[stream].append(copy)
            everything.append(copy)

    def add(phase, stream):
        kept = subsets(orders[stream][phase + 1 :])
        for slot, subset in enumerate(kept):
            block = flip_all(me, subset)

            def step(i, carry):
                rows = pl.ds(pl.multiple_of(i * 16, 16), 16)
                if phase == 0:
                    begin = pl.multiple_of(stream * half + i * 16, 16)
                    mine = grad_ref[block, pl.ds(begin, 16)]
                else:
                    mine = sums[stream][phase - 1][slot, rows]
                came = gots[stream][phase][slot, rows]
                total = mine.astype(jnp.float32) + came.astype(jnp.float32)
                if phase == phases - 1:
                    out_ref[pl.ds(pl.multiple_of(stream * half + i * 16, 16), 16)] = total
                else:
                    sums[stream][phase][slot, rows] = total.astype(jnp.bfloat16)
                return carry

            lax.fori_loop(0, half // 16, step, 0)

    start(0, 0)
    start(0, 1)
    smalls = []
    for step in range(1, number):
        peer = lax.rem(me + step, number)
        copy = pltpu.make_async_remote_copy(
            src_ref=small_ref,
            dst_ref=gathered_ref.at[me],
            send_sem=small_send.at[step],
            recv_sem=small_recv.at[step],
            device_id={"dp": peer},
            device_id_type=MESH,
        )
        copy.start()
        smalls.append(copy)
    gathered_ref[me] = small_ref[...]
    for phase in range(phases):
        for stream in range(2):
            for copy in flying[stream]:
                copy.wait_recv()
            add(phase, stream)
            if phase < phases - 1:
                start(phase + 1, stream)
    for copy in everything:
        copy.wait_send()
    for copy in smalls:
        copy.wait()


def scatter_grad(mesh, grad, small, collective_id):
    number = mesh.shape["dp"]
    rows, width = grad.shape[0] // number, grad.shape[1]
    blocks = grad.reshape(number, rows, width)
    phases = number.bit_length() - 1
    gots = [
        pltpu.VMEM((number >> (phase + 1), rows // 2, width), jnp.bfloat16)
        for phase in range(phases)
    ]
    return pl.pallas_call(
        functools.partial(scatter_kernel, number),
        out_shape=[
            jax.ShapeDtypeStruct((rows, width), jnp.float32),
            jax.ShapeDtypeStruct((number,) + small.shape, small.dtype),
        ],
        in_specs=[pl.BlockSpec(memory_space=pltpu.VMEM)] * 2,
        out_specs=[pl.BlockSpec(memory_space=pltpu.VMEM)] * 2,
        scratch_shapes=gots
        + gots
        + gots[:-1]
        + gots[:-1]
        + [
            pltpu.SemaphoreType.DMA((2, phases, number // 2)),
            pltpu.SemaphoreType.DMA((2, phases, number // 2)),
            pltpu.SemaphoreType.DMA((number,)),
            pltpu.SemaphoreType.DMA((number,)),
        ],
        compiler_params=pltpu.CompilerParams(
            collective_id=collective_id, has_side_effects=True, vmem_limit_bytes=VMEM_BYTES
        ),
    )(blocks, small)


def gather_kernel(number, mine_ref, out_ref, local_sem, send_sem, recv_sem):
    me = lax.axis_index("dp")
    rows = mine_ref.shape[0]
    greet(("dp",), (number,), me, number)
    orders = [order[::-1] for order in bit_orders(number)]
    half = rows // 2
    local = pltpu.make_async_copy(mine_ref, out_ref.at[me], local_sem)
    local.start()
    copies = []
    held = [[[]], [[]]]
    slot = [0, 0]
    waiting = [[], []]
    for phase in range(len(orders[0])):
        for stream, order in enumerate(orders):
            bit = order[phase]
            part = pl.ds(stream * half, half)
            for copy in waiting[stream]:
                copy.wait_recv()
            waiting[stream] = []
            for subset in held[stream]:
                block = flip_all(me, subset)
                source = out_ref.at[block, part] if subset else mine_ref.at[part]
                copy = pltpu.make_async_remote_copy(
                    src_ref=source,
                    dst_ref=out_ref.at[block, part],
                    send_sem=send_sem.at[stream, slot[stream]],
                    recv_sem=recv_sem.at[stream, slot[stream]],
                    device_id={"dp": flip(me, bit)},
                    device_id_type=MESH,
                )
                copy.start()
                copies.append(copy)
                waiting[stream].append(copy)
                slot[stream] += 1
            held[stream] = held[stream] + [subset + [bit] for subset in held[stream]]
    for stream in range(2):
        for copy in waiting[stream]:
            copy.wait_recv()
    for copy in copies:
        copy.wait_send()
    local.wait()


def gather_weights(mesh, mine, collective_id):
    number = mesh.shape["dp"]
    out = pl.pallas_call(
        functools.partial(gather_kernel, number),
        out_shape=jax.ShapeDtypeStruct((number,) + mine.shape, mine.dtype),
        in_specs=[pl.BlockSpec(memory_space=pltpu.VMEM)],
        out_specs=pl.BlockSpec(memory_space=pltpu.VMEM),
        scratch_shapes=[
            pltpu.SemaphoreType.DMA,
            pltpu.SemaphoreType.DMA((2, number)),
            pltpu.SemaphoreType.DMA((2, number)),
        ],
        compiler_params=pltpu.CompilerParams(
            collective_id=collective_id, has_side_effects=True, vmem_limit_bytes=VMEM_BYTES
        ),
    )(mine)
    return out.reshape(number * mine.shape[0], mine.shape[1])


def pool_kernel(slab_ref, index_ref, out_ref):
    slab = slab_ref[0]
    pairs, lanes = slab.shape
    batch, features = index_ref.shape[1:]
    pair_number = lax.broadcasted_iota(jnp.int32, (batch, pairs), 1)
    low = lax.broadcasted_iota(jnp.int32, (batch, lanes), 1) < lanes // 2
    for first in range(0, features, 2):
        halves = []
        for side in range(2):
            column = index_ref[0, :, first + side : first + side + 1]
            hot = jnp.where((column >> 1) == pair_number, 1.0, 0.0).astype(jnp.bfloat16)
            found = jnp.dot(hot, slab, preferred_element_type=jnp.float32)
            turned = pltpu.roll(found, lanes // 2, 1)
            halves.append(jnp.where((column & 1) == side, found, turned))
        start = first // 2 * lanes
        out_ref[:, start : start + lanes] = jnp.where(low, halves[0], halves[1]).astype(
            jnp.bfloat16
        )


def pool(slabs, indices):
    groups, pairs, lanes = slabs.shape
    batch, features = indices.shape[1:]
    return pl.pallas_call(
        pool_kernel,
        grid=(groups,),
        out_shape=jax.ShapeDtypeStruct((groups * batch, features * lanes // 2), jnp.bfloat16),
        in_specs=[
            pl.BlockSpec((1, pairs, lanes), lambda g: (g, 0, 0)),
            pl.BlockSpec((1, batch, features), lambda g: (g, 0, 0)),
        ],
        out_specs=pl.BlockSpec((batch, features * lanes // 2), lambda g: (g, 0)),
        compiler_params=pltpu.CompilerParams(vmem_limit_bytes=VMEM_BYTES),
    )(slabs, indices)


def slot_kernel(dact_ref, weight_ref, index_ref, turned_ref, out_ref, hot_ref, value_ref):
    pairs, lanes = out_ref.shape[1:]
    batch, features = index_ref.shape[1:]
    dpooled = lax.dot_general(
        dact_ref[...], weight_ref[...], (((1,), (1,)), ((), ())), preferred_element_type=jnp.float32
    )
    pair_number = lax.broadcasted_iota(jnp.int32, (pairs, batch), 0)
    upper = (lax.broadcasted_iota(jnp.int32, (batch, lanes), 1) >= lanes // 2).astype(jnp.int32)
    for feature in range(features):
        start = feature // 2 * lanes
        piece = dpooled[:, start : start + lanes]
        odd = index_ref[0, :, feature : feature + 1] & 1
        piece = jnp.where(odd == feature % 2, piece, pltpu.roll(piece, lanes // 2, 1))
        piece = jnp.where(upper == odd, piece, 0.0)
        high = piece.astype(jnp.bfloat16)
        rows = pl.ds(feature * batch, batch)
        value_ref[rows, 0:lanes] = high
        value_ref[rows, lanes : 2 * lanes] = (piece - high.astype(jnp.float32)).astype(jnp.bfloat16)
        line = turned_ref[0, feature : feature + 1, :] >> 1
        hot_ref[:, rows] = jnp.where(line == pair_number, 1.0, 0.0).astype(jnp.bfloat16)
    both = jnp.dot(hot_ref[...], value_ref[...], preferred_element_type=jnp.float32)
    out_ref[0] = (both[:, :lanes] + both[:, lanes:]).astype(jnp.bfloat16)


def slot_grads(dact, weight, indices, turned, pairs):
    groups, batch, features = indices.shape
    inputs, hidden = weight.shape
    lanes = 2 * inputs // features
    return pl.pallas_call(
        slot_kernel,
        grid=(groups,),
        out_shape=jax.ShapeDtypeStruct((groups, pairs, lanes), jnp.bfloat16),
        in_specs=[
            pl.BlockSpec((batch, hidden), lambda g: (g, 0)),
            pl.BlockSpec((inputs, hidden), lambda g: (0, 0)),
            pl.BlockSpec((1, batch, features), lambda g: (g, 0, 0)),
            pl.BlockSpec((1, features, batch), lambda g: (g, 0, 0)),
        ],
        out_specs=pl.BlockSpec((1, pairs, lanes), lambda g: (g, 0, 0)),
        scratch_shapes=[
            pltpu.VMEM((pairs, features * batch), jnp.bfloat16),
            pltpu.VMEM((features * batch, 2 * lanes), jnp.bfloat16),
        ],
        compiler_params=pltpu.CompilerParams(vmem_limit_bytes=VMEM_BYTES),
    )(dact, weight, indices, turned)


def table_kernel(arrived_ref, even_ref, odd_ref, out_ref):
    rows, width = out_ref.shape
    arrived = arrived_ref[...]
    count = arrived.shape[0]
    number = lax.broadcasted_iota(jnp.int32, (rows, count), 0) + pl.program_id(0) * rows
    even = jnp.where(even_ref[...] == number, 1.0, 0.0).astype(jnp.bfloat16)
    odd = jnp.where(odd_ref[...] == number, 1.0, 0.0).astype(jnp.bfloat16)
    first = jnp.dot(even, arrived, preferred_element_type=jnp.float32)
    second = jnp.dot(odd, arrived, preferred_element_type=jnp.float32)
    out_ref[...] = (first + pltpu.roll(second, width, 1))[:, :width]


def table_sums(arrived, even, odd, rows):
    count, lanes = arrived.shape
    tile = 512
    return pl.pallas_call(
        table_kernel,
        grid=(rows // tile,),
        out_shape=jax.ShapeDtypeStruct((rows, lanes // 2), jnp.float32),
        in_specs=[
            pl.BlockSpec((count, lanes), lambda r: (0, 0)),
            pl.BlockSpec((1, count), lambda r: (0, 0)),
            pl.BlockSpec((1, count), lambda r: (0, 0)),
        ],
        out_specs=pl.BlockSpec((tile, lanes // 2), lambda r: (r, 0)),
    )(arrived, even, odd)


def body(
    mesh,
    slab_values,
    row_ids,
    peer_counts,
    lookup_slots,
    labels,
    sample_weight,
    weight_in,
    bias_in,
    weight_out,
    dense_accum,
    table_rows,
    table_accum,
):
    peers = peer_counts.shape[1]
    capacity = row_ids.shape[2]
    emb_width = slab_values.shape[2] // capacity
    lanes = 2 * emb_width
    pairs = peers * capacity // 2
    index = slot_index(lookup_slots, peer_counts[0], capacity)
    slabs, indices = exchange(
        mesh, ("mp",), (slab_values.reshape(pairs, lanes), index), (False, False), 0
    )
    turned = jnp.swapaxes(indices, 1, 2)
    group = pool(slabs, indices)
    act = jnp.dot(group, weight_in, preferred_element_type=jnp.float32) + bias_in
    hidden = jax.nn.silu(act).astype(jnp.bfloat16)
    logit_part = jnp.dot(hidden, weight_out, preferred_element_type=jnp.float32)
    (logit_parts,) = exchange(mesh, ("mp",), (logit_part.reshape(-1, 128),), (False,), 1)
    logit = jnp.sum(logit_parts, axis=0).reshape(-1)
    dlogit = sample_weight * (jax.nn.sigmoid(logit) - labels.astype(jnp.float32))
    sigma = jax.nn.sigmoid(act)
    dact = (
        dlogit[:, None]
        * weight_out.astype(jnp.float32)[None, :]
        * sigma
        * (1.0 + act * (1.0 - sigma))
    ).astype(jnp.bfloat16)
    grad_in = lax.dot_general(
        group, dact, (((0,), (0,)), ((), ())), preferred_element_type=jnp.float32
    ).astype(jnp.bfloat16)
    grad_bias = jnp.sum(dact.astype(jnp.float32), axis=0)
    grad_out = jnp.sum(dlogit[:, None] * hidden.astype(jnp.float32), axis=0)
    small = jnp.concatenate([grad_bias.reshape(-1, 128), grad_out.reshape(-1, 128)])
    grad_rows, smalls = scatter_grad(mesh, grad_in, small, 2)
    partial = slot_grads(dact, weight_in, indices, turned, pairs)
    (parts,) = exchange(mesh, ("mp",), (partial,), (True,), 3)
    slot_grad = jnp.sum(parts.astype(jnp.float32), axis=0)
    first_group = (lax.axis_index("dp") == 0).astype(jnp.float32)
    small_sum = jnp.sum(smalls, axis=0)
    square = (
        jnp.sum(grad_rows * grad_rows)
        + first_group * jnp.sum(small_sum * small_sum)
        + jnp.sum(slot_grad * slot_grad)
    )
    arrived, arrived_rows, squares = exchange(
        mesh,
        ("dp", "mp"),
        (
            slot_grad.astype(jnp.bfloat16).reshape(peers, capacity // 2, lanes),
            row_ids.reshape(peers, 1, capacity),
            jnp.full((8, 128), square, jnp.float32),
        ),
        (True, True, False),
        4,
    )
    total = jnp.sum(squares[:, 0, 0])
    scale = clip_norm / jnp.maximum(jnp.sqrt(total), clip_norm)
    own_rows = dense_accum.shape[0]
    row_start = lax.axis_index("dp") * own_rows
    clipped = scale * grad_rows
    accum_new = dense_accum + clipped * clipped
    weight_part = lax.dynamic_slice_in_dim(weight_in, row_start, own_rows, 0).astype(jnp.float32)
    updated = (weight_part - dense_rate * clipped / (jnp.sqrt(accum_new) + adagrad_eps)).astype(
        jnp.bfloat16
    )
    weight_new = gather_weights(mesh, updated, 5)
    flat_rows = arrived_rows.reshape(-1, 2)
    received = scale * table_sums(
        arrived.reshape(pairs, lanes),
        flat_rows[:, 0].reshape(1, -1),
        flat_rows[:, 1].reshape(1, -1),
        table_rows.shape[0],
    )
    table_accum_new = table_accum + jnp.mean(received * received, axis=1)
    table_new = table_rows - table_rate * received / (
        jnp.sqrt(table_accum_new)[:, None] + adagrad_eps
    )
    return (weight_new, accum_new, table_new, table_accum_new)


def solution(mesh):
    placed = (
        P(("dp", "mp"), None, None),
        P(("dp", "mp"), None, None),
        P(("dp", "mp"), None),
        P(("dp", "mp"), None),
        P("dp"),
        P("dp"),
        P(None, "mp"),
        P("mp"),
        P("mp"),
        P("dp", "mp"),
        P(("dp", "mp"), None),
        P(("dp", "mp")),
    )
    return jax.shard_map(
        functools.partial(body, mesh),
        mesh=mesh,
        in_specs=placed,
        out_specs=(P(None, "mp"), P("dp", "mp"), P(("dp", "mp"), None), P(("dp", "mp"))),
        check_vma=False,
    )
```

time: 363 us -> 235 us (0.65)
  Pallas kernels: 0 us -> 164 us
  waiting for transfers between devices: 149 us -> 0 us
  blocking collectives: 71.8 us -> 0 us
  other arithmetic: 50 us -> 30.3 us
  local copies, waits for them, and re-layouts: 34.2 us -> 17.4 us
  between operations: 17.4 us -> 3.5 us
  matrix products: 31.3 us -> 19.1 us
  starting transfers between devices: 8.71 us -> 0 us
    pallas_call x0 -> x9, Pallas kernels: none -> 164 us  [the longest x4 68.4 us: exchange(): pl.pallas_call(functools.partial(exchange_kernel, axes, sizes, splits), o...]
    reduce_scatter x2 -> x0, waiting for transfers between devices: 86.4 us -> none  [the longest x1 50.6 us: body(): grad_rows = lax.psum_scatter(grad_in, 'dp', scatter_dimension=0, tiled=True)]
    psum x3 -> x0, blocking collectives: 71.8 us -> none  [the longest x1 39.3 us: body(): lax.psum(dense_square + jnp.sum(slot_grad * slot_grad), ('dp', 'mp'))]
    all_gather x2 -> x0, waiting for transfers between devices: 48.5 us -> none  [the longest x1 48.4 us: body(): group = lax.all_gather(pooled, 'mp', axis=0, tiled=True)]
    scatter-add x2 -> x0, other arithmetic: 29 us -> none  [the longest x1 22.5 us: body(): jax.ops.segment_sum(dpooled.reshape(batch * features, emb_width), index.r...]
    all_to_all x2 -> x0, waiting for transfers between devices: 14.1 us -> none  [the longest x1 8.03 us: body(): lax.all_to_all(outgoing, ('dp', 'mp'), split_axis=0, concat_axis=0, tiled...]
    gather x1 -> x0, local copies, waits for them, and re-layouts: 12.1 us -> none  [body(): pooled = slab_view[index].reshape(batch, features * emb_width)]
    dot_general x3 -> x1, matrix products: 11.2 us -> 1.79 us  [body(): logit_part = jnp.dot(hidden, weight_out, preferred_element_type=jnp.float32)]
  transfers between devices with their start and end apart: 6 -> 0, of which waited for: 5 -> 0; matrix products, arithmetic and copies ran while one was open for 15% -> 0% of each run, Pallas kernels for 0% -> 0%
where the time goes in v1:
time: 235 us; the launch traced here: 234 us
  Pallas kernels  164 us (70%)
  other arithmetic  30.3 us (13%)
  matrix products  19.1 us (8%)
  local copies, waits for them, and re-layouts  17.4 us (7%)
  between operations  3.5 us (1%)
    pallas_call x4, Pallas kernels, exchange(): pl.pallas_call(functools.partial(exchange_kernel, axes, sizes, splits), o...  68.4 us
    pallas_call x1, Pallas kernels, scatter_grad(): pl.pallas_call(functools.partial(scatter_kernel, number), out_shape=[jax....  30.5 us
    pallas_call x1, Pallas kernels, gather_weights(): pl.pallas_call(functools.partial(gather_kernel, number), out_shape=jax.Sh...  28.8 us
    pallas_call x1, Pallas kernels, pool(): pl.pallas_call(pool_kernel, grid=(groups,), out_shape=jax.ShapeDtypeStruc...  15.3 us
    pallas_call x1, Pallas kernels, slot_grads(): pl.pallas_call(slot_kernel, grid=(groups,), out_shape=jax.ShapeDtypeStruc...  14.9 us
    unnamed x28, local copies, waits for them, and re-layouts  11.9 us
    dot_general x1, matrix products, body(): jnp.dot(group, weight_in, preferred_element_type=jnp.float32) + bias_in  11.1 us
    reduce_sum x1, other arithmetic, body(): grad_bias = jnp.sum(dact.astype(jnp.float32), axis=0)  7.63 us

profile of v1, /device:TPU:0, one launch (start us, length us, event | category | flops | bytes accessed | tf_op | source)
XLA Modules:
  0.0 234.4 jit_solution(2761470996710762101)
XLA Ops:
  0.6 0.7 copy.36
  1.6 0.9 convert_reduce_fusion.2
  4.9 1.6 reshape.76.refs_0_
  6.5 25.0 %shard_map.147 = (bf16[4,512,128]{2,1,0:T(8,128)(2,1)}, s32[4,256,16]{2,1,0:T(8,128)}) custom-call(bf16[512,128]{1,0:T(8,128)(2,1)} %reshape.76.refs_0_, s32[256,16]{1,0:T(8,128)} %sub.19.refs_1_), custom_call_target="tpu_custom_call" | custom-call | tf_op jit(solution)/shard_map/pallas_call | solution.py:90
  31.5 15.3 %shard_map.148 = bf16[1024,1024]{1,0:T(8,128)(2,1)} custom-call(bf16[4,512,128]{2,1,0:T(8,128)(2,1)} %get-tuple-element.11.slab_ref, s32[4,256,16]{2,1,0:T(8,128)} %get-tuple-element.12.index_ref), custom_call_target="tpu_custom_call" | custom-call | tf_op jit(solution)/shard_map/pallas_call | solution.py:330
  46.8 11.1 %multiply_convert_fusion.1 = (bf16[1024,2048]{1,0:T(8,128)(2,1)S(1)}, f32[1024,2048]{1,0:T(8,128)}) fusion(f32[2048]{0:T(1024)S(1)} %copy-done.9, bf16[1024,1024]{1,0:T(8,128)(2,1)} %shard_map.148, bf16[1024,2048]{1,0:T(8,128)(2,1)} %weight_ref.1), kind=kOutput, calls=%fused_computation.3 | convolution fusion | flops 4307550208 | bytes 18882560 | tf_op jit(solution)/shard_map/dot_general | solution.py:444
  57.9 2.0 copy-done
  59.9 1.8 fusion.1
  61.7 11.5 %shard_map.149 = f32[4,8,128]{2,1,0:T(8,128)} custom-call(f32[8,128]{1,0:T(8,128)} %bitcast.33), custom_call_target="tpu_custom_call" | custom-call | tf_op jit(solution)/shard_map/pallas_call | solution.py:90
  73.3 0.7 reduce_sum.110
  74.0 7.6 %convert_reduce_fusion = (f32[2048]{0:T(1024)S(1)}, bf16[1024,2048]{1,0:T(8,128)(2,1)S(1)}, f32[2048]{0:T(1024)S(1)}) fusion(f32[1024,2048]{1,0:T(8,128)} %get-tuple-element.46, f32[2048]{0:T(1024)S(1)} %copy-done.9, f32[2048]{0:T(1024)S(1)} %convert_element_type.45, f32[1024]{0:T(1024)S(1)} %fusion, bf16[1024,2048]{1,0:T(8,128)(2,1)} %copy-done), kind=kLoop, calls=%fused_computation.1 | loop fusion | flops 33550336 | bytes 16814080 | tf_op jit(solution)/shard_map/reduce_sum | solution.py:460
  82.3 6.2 %convolution_convert_fusion = bf16[1024,2048]{1,0:T(8,128)(2,1)} fusion(bf16[1024,1024]{1,0:T(8,128)(2,1)S(1)} %copy-done.5, bf16[1024,2048]{1,0:T(8,128)(2,1)S(1)} %get-tuple-element.41.dact_ref), kind=kOutput, calls=%fused_computation.5 | convolution fusion | flops 4297064448 | bytes 10485760 | tf_op jit(solution)/shard_map/dot_general | solution.py:457
  88.6 30.5 %shard_map.152 = (f32[128,2048]{1,0:T(8,128)}, f32[8,32,128]{2,1,0:T(8,128)}) custom-call(bf16[8,128,2048]{2,1,0:T(8,128)(2,1)} %bitcast.27, f32[32,128]{1,0:T(8,128)} %pad_maximum_fusion.small_ref), custom_call_target="tpu_custom_call" | custom-call | tf_op jit(solution)/shard_map/pallas_call | solution.py:221
  119.0 0.9 reduce_sum.115
  121.2 2.1 multiply_reduce_fusion.2
  124.0 0.8 copy.39
  124.8 14.9 %shard_map.150.refs_0_ = bf16[4,512,128]{2,1,0:T(8,128)(2,1)} custom-call(bf16[1024,2048]{1,0:T(8,128)(2,1)} %copy-done.2, bf16[1024,2048]{1,0:T(8,128)(2,1)} %weight_ref.1, s32[4,256,16]{2,1,0:T(8,128)} %get-tuple-element.12.index_ref, s32[4,16,256]{2,1,0:T(8,128)} %bitcast.29), custom_call_target="tpu_custom_call" | custom-call | tf_op jit(solution)/shard_map/pallas_call | solution.py:371
  139.7 14.2 %shard_map.151 = bf16[4,512,128]{2,1,0:T(8,128)(2,1)} custom-call(bf16[4,512,128]{2,1,0:T(8,128)(2,1)} %shard_map.150.refs_0_), custom_call_target="tpu_custom_call" | custom-call | tf_op jit(solution)/shard_map/pallas_call | solution.py:90
  153.8 1.1 convert_reduce_fusion.1
  155.0 1.3 multiply_reduce_fusion.3
  157.5 17.7 %shard_map.153 = (bf16[32,16,128]{2,1,0:T(8,128)(2,1)}, s32[32,1,32]{2,1,0:T(1,128)}, f32[32,8,128]{2,1,0:T(8,128)}) custom-call(bf16[32,16,128]{2,1,0:T(8,128)(2,1)} %bitcast.28, s32[32,1,32]{2,1,0:T(1,128)} %bitcast.34, f32[8,128]{1,0:T(8,128)} %broadcast_in_dim.12.refs_2_), custom_call_target="tpu_custom_call" | custom-call | tf_op jit(solution)/shard_map/pallas_call | solution.py:90
  175.7 1.4 reduce.9
  177.3 0.9 slice_reduce_fusion
  178.1 6.3 %shard_map.155 = f32[4096,64]{1,0:T(8,128)} custom-call(bf16[512,128]{1,0:T(8,128)(2,1)} %bitcast.30, s32[1,512]{1,0:T(1,128)} %bitcast.36, s32[1,512]{1,0:T(1,128)} %bitcast.35), custom_call_target="tpu_custom_call" | custom-call | tf_op jit(solution)/shard_map/pallas_call | solution.py:405
  184.4 1.7 slice_reduce_fusion.2
  186.9 2.2 multiply_reduce_fusion.1
  189.7 1.9 copy.40
  191.6 3.0 %divide_subtract_fusion = f32[4096,64]{1,0:T(8,128)} fusion(f32[4096,64]{1,0:T(8,128)} %copy.40, f32[4096,64]{1,0:T(8,128)S(1)} %copy-done.1, f32[4096]{0:T(1024)S(1)} %get-tuple-element.36, f32[]{:T(128)S(6)} %div.34), kind=kLoop, calls=%fused_computation.6 | loop fusion | flops 1048576 | bytes 3162116 | tf_op jit(solution)/shard_map/sub | solution.py:504
  194.6 3.1 %copy.41 = f32[4096,64]{0,1:T(8,128)} copy(f32[4096,64]{1,0:T(8,128)} %divide_subtract_fusion) | data formatting | bytes 2097152
  197.8 3.1 %subtract_convert_fusion = (bf16[128,2048]{1,0:T(8,128)(2,1)}, f32[128,2048]{1,0:T(8,128)}) fusion(f32[128,2048]{1,0:T(8,128)S(1)} %copy-done.4, f32[]{:T(128)S(6)} %div.34, bf16[1024,2048]{1,0:T(8,128)(2,1)} %weight_ref.1, s32[]{:T(128)S(6)} %select_n.7, f32[128,2048]{1,0:T(8,128)} %param.21), kind=kLoop, calls=%fused_computation.8 | loop fusion | flops 2359296 | bytes 4194312 | tf_op jit(solution)/shard_map/convert_element_type | solution.py:492
  200.9 28.8 %shard_map.154 = bf16[8,128,2048]{2,1,0:T(8,128)(2,1)} custom-call(bf16[128,2048]{1,0:T(8,128)(2,1)} %get-tuple-element.38.mine_ref), custom_call_target="tpu_custom_call" | custom-call | tf_op jit(solution)/shard_map/pallas_call | solution.py:290
  229.7 4.8 %copy.43 = bf16[1024,2048]{1,0:T(8,128)(2,1)} copy(bf16[1024,2048]{1,0:T(8,128)(2,1)} %bitcast.26) | data formatting | bytes 8388608
  (40 shorter events, 5.8 us)
Async XLA Ops:
  0.6 46.1 %copy-start.9 = (f32[2048]{0:T(1024)S(1)}, f32[2048]{0:T(1024)}, u32[]{:S(2)}) copy-start(f32[2048]{0:T(1024)} %param.19) | copy-start | bytes 24580
  46.8 11.2 %copy-start.7 = (bf16[2048]{0:T(1024)(128)(2,1)S(1)}, bf16[2048]{0:T(1024)(128)(2,1)}, u32[]{:S(2)}) copy-start(bf16[2048]{0:T(1024)(128)(2,1)} %param.20) | copy-start | bytes 12292
  57.9 2.0 copy-start
  57.9 16.1 %copy-start.10 = (f32[1024]{0:T(1024)S(1)}, f32[1024]{0:T(1024)}, u32[]{:S(2)}) copy-start(f32[1024]{0:T(1024)} %param.17) | copy-start | bytes 12292
  57.9 16.1 %copy-start.11 = (s32[1024]{0:T(1024)S(1)}, s32[1024]{0:T(1024)}, u32[]{:S(2)}) copy-start(s32[1024]{0:T(1024)} %param.16) | copy-start | bytes 12292
  74.0 8.3 %copy-start.5 = (bf16[1024,1024]{1,0:T(8,128)(2,1)S(1)}, bf16[1024,1024]{1,0:T(8,128)(2,1)}, u32[]{:S(2)}) copy-start(bf16[1024,1024]{1,0:T(8,128)(2,1)} %shard_map.148) | copy-start | bytes 6291460
  81.7 6.9 %copy-start.2 = (bf16[1024,2048]{1,0:T(8,128)(2,1)}, bf16[1024,2048]{1,0:T(8,128)(2,1)S(1)}, u32[]{:S(2)}) copy-start(bf16[1024,2048]{1,0:T(8,128)(2,1)S(1)} %get-tuple-element.41.dact_ref) | copy-start | bytes 12582916
  88.6 35.4 %copy-start.3 = (s32[4,256,16]{2,1,0:T(8,128)S(1)}, s32[4,256,16]{2,1,0:T(8,128)}, u32[]{:S(2)}) copy-start(s32[4,256,16]{2,1,0:T(8,128)} %get-tuple-element.12.index_ref) | copy-start | bytes 196612
  139.7 49.4 %copy-start.8 = (f32[4096]{0:T(1024)S(1)}, f32[4096]{0:T(1024)}, u32[]{:S(2)}) copy-start(f32[4096]{0:T(1024)} %param.23) | copy-start | bytes 49156
  139.7 50.0 %copy-start.6 = (f32[4096,64]{0,1:T(8,128)S(1)}, f32[4096,64]{0,1:T(8,128)}, u32[]{:S(2)}) copy-start(f32[4096,64]{0,1:T(8,128)} %param.22) | copy-start | bytes 3145732
  184.4 7.2 %copy-start.1 = (f32[4096,64]{1,0:T(8,128)S(1)}, f32[4096,64]{1,0:T(8,128)}, u32[]{:S(2)}) copy-start(f32[4096,64]{1,0:T(8,128)} %shard_map.155) | copy-start | bytes 3145732
  191.6 6.1 %copy-start.4 = (f32[128,2048]{1,0:T(8,128)S(1)}, f32[128,2048]{1,0:T(8,128)}, u32[]{:S(2)}) copy-start(f32[128,2048]{1,0:T(8,128)} %get-tuple-element.13) | copy-start | bytes 3145732

commit v2 on v1

--- a/solution.py
+++ b/solution.py
@@ -246,7 +246,7 @@
     me = lax.axis_index("dp")
     rows = mine_ref.shape[0]
     greet(("dp",), (number,), me, number)
-    orders = [order[::-1] for order in bit_orders(number)]
+    orders = [order[:0:-1] for order in bit_orders(number)]
     half = rows // 2
     local = pltpu.make_async_copy(mine_ref, out_ref.at[me], local_sem)
     local.start()
@@ -254,32 +254,39 @@
     held = [[[]], [[]]]
     slot = [0, 0]
     waiting = [[], []]
-    for phase in range(len(orders[0])):
+    across = []
+
+    def send(stream, subset, bit):
+        part = pl.ds(stream * half, half)
+        block = flip_all(me, subset)
+        copy = pltpu.make_async_remote_copy(
+            src_ref=out_ref.at[block, part] if subset else mine_ref.at[part],
+            dst_ref=out_ref.at[block, part],
+            send_sem=send_sem.at[stream, slot[stream]],
+            recv_sem=recv_sem.at[stream, slot[stream]],
+            device_id={"dp": flip(me, bit)},
+            device_id_type=MESH,
+        )
+        copy.start()
+        copies.append(copy)
+        slot[stream] += 1
+        return copy
+
+    fresh = [[[]], [[]]]
+    for phase in range(len(orders[0]) + 1):
         for stream, order in enumerate(orders):
-            bit = order[phase]
-            part = pl.ds(stream * half, half)
             for copy in waiting[stream]:
                 copy.wait_recv()
             waiting[stream] = []
-            for subset in held[stream]:
-                block = flip_all(me, subset)
-                source = out_ref.at[block, part] if subset else mine_ref.at[part]
-                copy = pltpu.make_async_remote_copy(
-                    src_ref=source,
-                    dst_ref=out_ref.at[block, part],
-                    send_sem=send_sem.at[stream, slot[stream]],
-                    recv_sem=recv_sem.at[stream, slot[stream]],
-                    device_id={"dp": flip(me, bit)},
-                    device_id_type=MESH,
-                )
-                copy.start()
-                copies.append(copy)
-                waiting[stream].append(copy)
-                slot[stream] += 1
-            held[stream] = held[stream] + [subset + [bit] for subset in held[stream]]
-    for stream in range(2):
-        for copy in waiting[stream]:
-            copy.wait_recv()
+            if phase < len(order):
+                bit = order[phase]
+                waiting[stream] = [send(stream, subset, bit) for subset in held[stream]]
+            across.extend(send(stream, subset, 0) for subset in fresh[stream])
+            if phase < len(order):
+                fresh[stream] = [subset + [bit] for subset in held[stream]]
+                held[stream] = held[stream] + fresh[stream]
+    for copy in across:
+        copy.wait_recv()
     for copy in copies:
         copy.wait_send()
     local.wait()
@@ -304,18 +311,23 @@
     return out.reshape(number * mine.shape[0], mine.shape[1])
 
 
-def pool_kernel(slab_ref, index_ref, out_ref):
+def pool_kernel(slab_ref, index_ref, out_ref, hot_ref, found_ref):
     slab = slab_ref[0]
     pairs, lanes = slab.shape
     batch, features = index_ref.shape[1:]
     pair_number = lax.broadcasted_iota(jnp.int32, (batch, pairs), 1)
     low = lax.broadcasted_iota(jnp.int32, (batch, lanes), 1) < lanes // 2
+    for feature in range(features):
+        column = index_ref[0, :, feature : feature + 1] >> 1
+        hot_ref[pl.ds(feature * batch, batch), :] = jnp.where(
+            column == pair_number, 1.0, 0.0
+        ).astype(jnp.bfloat16)
+    found_ref[...] = jnp.dot(hot_ref[...], slab, preferred_element_type=jnp.float32)
     for first in range(0, features, 2):
         halves = []
         for side in range(2):
             column = index_ref[0, :, first + side : first + side + 1]
-            hot = jnp.where((column >> 1) == pair_number, 1.0, 0.0).astype(jnp.bfloat16)
-            found = jnp.dot(hot, slab, preferred_element_type=jnp.float32)
+            found = found_ref[pl.ds((first + side) * batch, batch), :]
             turned = pltpu.roll(found, lanes // 2, 1)
             halves.append(jnp.where((column & 1) == side, found, turned))
         start = first // 2 * lanes
@@ -336,6 +348,10 @@
             pl.BlockSpec((1, batch, features), lambda g: (g, 0, 0)),
         ],
         out_specs=pl.BlockSpec((batch, features * lanes // 2), lambda g: (g, 0)),
+        scratch_shapes=[
+            pltpu.VMEM((features * batch, pairs), jnp.bfloat16),
+            pltpu.VMEM((features * batch, lanes), jnp.float32),
+        ],
         compiler_params=pltpu.CompilerParams(vmem_limit_bytes=VMEM_BYTES),
     )(slabs, indices)
 
@@ -436,10 +452,10 @@
     lanes = 2 * emb_width
     pairs = peers * capacity // 2
     index = slot_index(lookup_slots, peer_counts[0], capacity)
-    slabs, indices = exchange(
-        mesh, ("mp",), (slab_values.reshape(pairs, lanes), index), (False, False), 0
-    )
-    turned = jnp.swapaxes(indices, 1, 2)
+    slabs, turned = exchange(
+        mesh, ("mp",), (slab_values.reshape(pairs, lanes), index.T), (False, False), 0
+    )
+    indices = jnp.swapaxes(turned, 1, 2)
     group = pool(slabs, indices)
     act = jnp.dot(group, weight_in, preferred_element_type=jnp.float32) + bias_in
     hidden = jax.nn.silu(act).astype(jnp.bfloat16)

time: 235 us -> 218 us (0.928)
  Pallas kernels: 164 us -> 146 us
    pallas_call x4, Pallas kernels: 68.4 us -> 58.3 us  [exchange(): pl.pallas_call(functools.partial(exchange_kernel, axes, sizes, splits), o...]
    pallas_call x1, Pallas kernels: 15.3 us -> 8.35 us  [pool(): pl.pallas_call(pool_kernel, grid=(groups,), out_shape=jax.ShapeDtypeStruc...]
    unnamed x28 -> x26, local copies, waits for them, and re-layouts: 11.9 us -> 11.9 us
where the time goes in v2:
time: 218 us; the launch traced here: 217 us
  Pallas kernels  146 us (67%)
  other arithmetic  30.2 us (14%)
  matrix products  19.1 us (9%)
  local copies, waits for them, and re-layouts  18.2 us (8%)
  between operations  3.49 us (2%)
    pallas_call x4, Pallas kernels, exchange(): pl.pallas_call(functools.partial(exchange_kernel, axes, sizes, splits), o...  58.3 us
    pallas_call x1, Pallas kernels, scatter_grad(): pl.pallas_call(functools.partial(scatter_kernel, number), out_shape=[jax....  30.6 us
    pallas_call x1, Pallas kernels, gather_weights(): pl.pallas_call(functools.partial(gather_kernel, number), out_shape=jax.Sh...  27.3 us
    pallas_call x1, Pallas kernels, slot_grads(): pl.pallas_call(slot_kernel, grid=(groups,), out_shape=jax.ShapeDtypeStruc...  14.9 us
    unnamed x26, local copies, waits for them, and re-layouts  11.9 us
    dot_general x1, matrix products, body(): jnp.dot(group, weight_in, preferred_element_type=jnp.float32) + bias_in  11.1 us
    pallas_call x1, Pallas kernels, pool(): pl.pallas_call(pool_kernel, grid=(groups,), out_shape=jax.ShapeDtypeStruc...  8.35 us
    reduce_sum x1, other arithmetic, body(): grad_bias = jnp.sum(dact.astype(jnp.float32), axis=0)  7.63 us

profile of v2, /device:TPU:0, one launch (start us, length us, event | category | flops | bytes accessed | tf_op | source)
XLA Modules:
  0.0 216.8 jit_solution(16643391426786672261)
XLA Ops:
  0.6 0.7 copy.28
  1.6 0.9 convert_reduce_fusion.2
  3.3 1.3 subtract_bitcast_fusion.refs_1_
  4.6 1.6 reshape.76.refs_0_
  6.2 17.4 %shard_map.147 = (bf16[4,512,128]{2,1,0:T(8,128)(2,1)}, s32[4,16,256]{2,1,0:T(8,128)}) custom-call(bf16[512,128]{1,0:T(8,128)(2,1)} %reshape.76.refs_0_, s32[16,256]{1,0:T(8,128)} %subtract_bitcast_fusion.refs_1_), custom_call_target="tpu_custom_call" | custom-call | tf_op jit(solution)/shard_map/pallas_call | solution.py:90
  23.6 1.8 copy.29
  25.5 8.4 %shard_map.148 = bf16[1024,1024]{1,0:T(8,128)(2,1)} custom-call(bf16[4,512,128]{2,1,0:T(8,128)(2,1)} %get-tuple-element.11.slab_ref, s32[4,256,16]{2,1,0:T(8,128)} %bitcast.29), custom_call_target="tpu_custom_call" | custom-call | tf_op jit(solution)/shard_map/pallas_call | solution.py:342
  33.8 11.1 %multiply_convert_fusion.1 = (bf16[1024,2048]{1,0:T(8,128)(2,1)S(1)}, f32[1024,2048]{1,0:T(8,128)}) fusion(f32[2048]{0:T(1024)S(1)} %copy-done.8, bf16[1024,1024]{1,0:T(8,128)(2,1)} %shard_map.148, bf16[1024,2048]{1,0:T(8,128)(2,1)} %weight_ref.1), kind=kOutput, calls=%fused_computation.3 | convolution fusion | flops 4307550208 | bytes 18882560 | tf_op jit(solution)/shard_map/dot_general | solution.py:460
  45.0 2.0 copy-done
  47.0 1.8 fusion.1
  48.8 9.0 %shard_map.149 = f32[4,8,128]{2,1,0:T(8,128)} custom-call(f32[8,128]{1,0:T(8,128)} %bitcast.36), custom_call_target="tpu_custom_call" | custom-call | tf_op jit(solution)/shard_map/pallas_call | solution.py:90
  58.6 7.6 %convert_reduce_fusion = (f32[2048]{0:T(1024)S(1)}, bf16[1024,2048]{1,0:T(8,128)(2,1)S(1)}, f32[2048]{0:T(1024)S(1)}) fusion(f32[1024,2048]{1,0:T(8,128)} %get-tuple-element.42, f32[2048]{0:T(1024)S(1)} %copy-done.8, f32[2048]{0:T(1024)S(1)} %convert_element_type.45, f32[1024]{0:T(1024)S(1)} %fusion, bf16[1024,2048]{1,0:T(8,128)(2,1)} %copy-done), kind=kLoop, calls=%fused_computation.1 | loop fusion | flops 33550336 | bytes 16814080 | tf_op jit(solution)/shard_map/reduce_sum | solution.py:476
  66.9 6.2 %convolution_convert_fusion = bf16[1024,2048]{1,0:T(8,128)(2,1)} fusion(bf16[1024,1024]{1,0:T(8,128)(2,1)S(1)} %copy-done.4, bf16[1024,2048]{1,0:T(8,128)(2,1)S(1)} %get-tuple-element.37.dact_ref), kind=kOutput, calls=%fused_computation.5 | convolution fusion | flops 4297064448 | bytes 10485760 | tf_op jit(solution)/shard_map/dot_general | solution.py:473
  73.1 30.6 %shard_map.152 = (f32[128,2048]{1,0:T(8,128)}, f32[8,32,128]{2,1,0:T(8,128)}) custom-call(bf16[8,128,2048]{2,1,0:T(8,128)(2,1)} %bitcast.31, f32[32,128]{1,0:T(8,128)} %pad_maximum_fusion.small_ref), custom_call_target="tpu_custom_call" | custom-call | tf_op jit(solution)/shard_map/pallas_call | solution.py:221
  103.7 0.9 reduce_sum.115
  105.9 2.1 multiply_reduce_fusion.2
  108.6 14.9 %shard_map.150.refs_0_ = bf16[4,512,128]{2,1,0:T(8,128)(2,1)} custom-call(bf16[1024,2048]{1,0:T(8,128)(2,1)} %copy-done.2, bf16[1024,2048]{1,0:T(8,128)(2,1)} %weight_ref.1, s32[4,256,16]{2,1,0:T(8,128)} %bitcast.30, s32[4,16,256]{2,1,0:T(8,128)} %get-tuple-element.12.turned_ref), custom_call_target="tpu_custom_call" | custom-call | tf_op jit(solution)/shard_map/pallas_call | solution.py:387
  123.6 14.1 %shard_map.151 = bf16[4,512,128]{2,1,0:T(8,128)(2,1)} custom-call(bf16[4,512,128]{2,1,0:T(8,128)(2,1)} %shard_map.150.refs_0_), custom_call_target="tpu_custom_call" | custom-call | tf_op jit(solution)/shard_map/pallas_call | solution.py:90
  137.7 1.1 convert_reduce_fusion.1
  138.9 1.3 multiply_reduce_fusion.3
  141.4 17.7 %shard_map.153 = (bf16[32,16,128]{2,1,0:T(8,128)(2,1)}, s32[32,1,32]{2,1,0:T(1,128)}, f32[32,8,128]{2,1,0:T(8,128)}) custom-call(bf16[32,16,128]{2,1,0:T(8,128)(2,1)} %bitcast.32, s32[32,1,32]{2,1,0:T(1,128)} %bitcast.37, f32[8,128]{1,0:T(8,128)} %broadcast_in_dim.12.refs_2_), custom_call_target="tpu_custom_call" | custom-call | tf_op jit(solution)/shard_map/pallas_call | solution.py:90
  159.6 1.4 reduce.9
  161.1 0.9 slice_reduce_fusion
  162.0 6.3 %shard_map.155 = f32[4096,64]{1,0:T(8,128)} custom-call(bf16[512,128]{1,0:T(8,128)(2,1)} %bitcast.33, s32[1,512]{1,0:T(1,128)} %bitcast.39, s32[1,512]{1,0:T(1,128)} %bitcast.38), custom_call_target="tpu_custom_call" | custom-call | tf_op jit(solution)/shard_map/pallas_call | solution.py:421
  168.3 1.7 slice_reduce_fusion.2
  170.8 2.2 %multiply_reduce_fusion.1 = f32[4096]{0:T(1024)S(1)} fusion(f32[4096,64]{1,0:T(8,128)} %shard_map.155, f32[]{:T(128)S(6)} %div.34), kind=kLoop, calls=%fused_computation.7 | loop fusion | flops 782336 | bytes 1064964 | tf_op jit(solution)/shard_map/reduce_sum | solution.py:519
  173.6 1.9 copy.30
  175.5 3.0 %divide_subtract_fusion = f32[4096,64]{1,0:T(8,128)} fusion(f32[4096,64]{1,0:T(8,128)} %copy.30, f32[4096,64]{1,0:T(8,128)S(1)} %copy-done.1, f32[4096]{0:T(1024)S(1)} %get-tuple-element.32, f32[]{:T(128)S(6)} %div.34), kind=kLoop, calls=%fused_computation.6 | loop fusion | flops 1048576 | bytes 3162116 | tf_op jit(solution)/shard_map/sub | solution.py:520
  178.5 3.1 %copy.31 = f32[4096,64]{0,1:T(8,128)} copy(f32[4096,64]{1,0:T(8,128)} %divide_subtract_fusion) | data formatting | bytes 2097152
  181.7 3.1 %subtract_convert_fusion = (bf16[128,2048]{1,0:T(8,128)(2,1)}, f32[128,2048]{1,0:T(8,128)}) fusion(f32[128,2048]{1,0:T(8,128)S(1)} %copy-done.3, f32[]{:T(128)S(6)} %div.34, bf16[1024,2048]{1,0:T(8,128)(2,1)} %weight_ref.1, s32[]{:T(128)S(6)} %select_n.7, f32[128,2048]{1,0:T(8,128)} %param.21), kind=kLoop, calls=%fused_computation.8 | loop fusion | flops 2359296 | bytes 4194312 | tf_op jit(solution)/shard_map/convert_element_type | solution.py:508
  184.7 27.3 %shard_map.154 = bf16[8,128,2048]{2,1,0:T(8,128)(2,1)} custom-call(bf16[128,2048]{1,0:T(8,128)(2,1)} %get-tuple-element.34.mine_ref), custom_call_target="tpu_custom_call" | custom-call | tf_op jit(solution)/shard_map/pallas_call | solution.py:297
  212.0 4.8 %copy.33 = bf16[1024,2048]{1,0:T(8,128)(2,1)} copy(bf16[1024,2048]{1,0:T(8,128)(2,1)} %bitcast.28) | data formatting | bytes 8388608
  (35 shorter events, 4.9 us)
Async XLA Ops:
  0.6 33.2 %copy-start.8 = (f32[2048]{0:T(1024)S(1)}, f32[2048]{0:T(1024)}, u32[]{:S(2)}) copy-start(f32[2048]{0:T(1024)} %param.19) | copy-start | bytes 24580
  33.8 11.1 %copy-start.6 = (bf16[2048]{0:T(1024)(128)(2,1)S(1)}, bf16[2048]{0:T(1024)(128)(2,1)}, u32[]{:S(2)}) copy-start(bf16[2048]{0:T(1024)(128)(2,1)} %param.20) | copy-start | bytes 12292
  45.0 2.0 copy-start
  45.0 13.6 %copy-start.9 = (f32[1024]{0:T(1024)S(1)}, f32[1024]{0:T(1024)}, u32[]{:S(2)}) copy-start(f32[1024]{0:T(1024)} %param.17) | copy-start | bytes 12292
  45.0 13.6 %copy-start.10 = (s32[1024]{0:T(1024)S(1)}, s32[1024]{0:T(1024)}, u32[]{:S(2)}) copy-start(s32[1024]{0:T(1024)} %param.16) | copy-start | bytes 12292
  58.6 8.3 %copy-start.4 = (bf16[1024,1024]{1,0:T(8,128)(2,1)S(1)}, bf16[1024,1024]{1,0:T(8,128)(2,1)}, u32[]{:S(2)}) copy-start(bf16[1024,1024]{1,0:T(8,128)(2,1)} %shard_map.148) | copy-start | bytes 6291460
  66.2 6.9 %copy-start.2 = (bf16[1024,2048]{1,0:T(8,128)(2,1)}, bf16[1024,2048]{1,0:T(8,128)(2,1)S(1)}, u32[]{:S(2)}) copy-start(bf16[1024,2048]{1,0:T(8,128)(2,1)S(1)} %get-tuple-element.37.dact_ref) | copy-start | bytes 12582916
  123.6 49.4 %copy-start.7 = (f32[4096]{0:T(1024)S(1)}, f32[4096]{0:T(1024)}, u32[]{:S(2)}) copy-start(f32[4096]{0:T(1024)} %param.23) | copy-start | bytes 49156
  123.6 50.0 %copy-start.5 = (f32[4096,64]{0,1:T(8,128)S(1)}, f32[4096,64]{0,1:T(8,128)}, u32[]{:S(2)}) copy-start(f32[4096,64]{0,1:T(8,128)} %param.22) | copy-start | bytes 3145732
  168.3 7.2 %copy-start.1 = (f32[4096,64]{1,0:T(8,128)S(1)}, f32[4096,64]{1,0:T(8,128)}, u32[]{:S(2)}) copy-start(f32[4096,64]{1,0:T(8,128)} %shard_map.155) | copy-start | bytes 3145732
  175.5 6.1 %copy-start.3 = (f32[128,2048]{1,0:T(8,128)S(1)}, f32[128,2048]{1,0:T(8,128)}, u32[]{:S(2)}) copy-start(f32[128,2048]{1,0:T(8,128)} %get-tuple-element.13) | copy-start | bytes 3145732
